TPU v7x, 32 devices: a whole 2x2x4 slice. The times are simulated.
32 devices in a mesh: shard: 2 (over core), cols: 4 (over y, x), job: 4 (over z).
Axes of the slice: x: 2, y: 2, z: 4, core: 2. Of those that a mesh axis runs over, the one named last changes fastest.
Arguments:
- one_query: float32 [16384, 4096], P(('job', 'shard'), 'cols'), parts along dimension 0, may hold values from -0.125 to 0.125
- other_query: float32 [16384, 4096], P(('job', 'shard'), 'cols'), parts along dimension 0, may hold values from -0.09375 to 0.09375
- one_key: float32 [16384, 1024], P(('job', 'shard'), 'cols'), parts along dimension 0, may hold values from -0.125 to 0.125
- other_key: float32 [16384, 1024], P(('job', 'shard'), 'cols'), parts along dimension 0, may hold values from -0.09375 to 0.09375
- one_value: float32 [16384, 1024], P(('job', 'shard'), 'cols'), parts along dimension 0, may hold values from -0.125 to 0.125
- other_value: float32 [16384, 1024], P(('job', 'shard'), 'cols'), parts along dimension 0, may hold values from -0.09375 to 0.09375
- mix_share: float32 [16384], P(('job', 'shard')), parts along dimension 0, may hold values from 0.2 to 0.8
- norm_gain: float32 [16384], P(('job', 'shard')), parts along dimension 0, may hold values from 0.25 to 1.75
Outputs:
- final_query: bfloat16 [16384, 4096], P('job', 'cols'), parts along dimension 0
- final_key: bfloat16 [16384, 1024], P('job', 'cols'), parts along dimension 0
- final_value: bfloat16 [16384, 1024], P('job', 'cols'), parts along dimension 0
- scale_query: float32 [16384], P(('job', 'cols')), parts along dimension 0
- scale_key: float32 [4096], P(('job', 'cols')), parts along dimension 0
- scale_value: float32 [4096], P(('job', 'cols')), parts along dimension 0
There are 4 independent parts, one for each index of `job`. A program takes and returns all parts, laid end to end along the dimension named above; each array names one. Nothing has to cross between parts.
All inputs are finite; a program needn't handle non-finite values. Where the computation divides by a largest or mean magnitude, that divisor is 1e-20 or more.
Results may differ from a plain program's by a relative error of at most 0.001.
Values may be sent and summed in bfloat16 or wider, within the bound.
No kernel may reach another device: no remote copies, remote signals or barrier semaphores. Data moves between devices by JAX's collectives and lax.ppermute only.
A program may use at most 128 MiB of HBM per device.

v0:
```python
import jax
import jax.numpy as jnp
from jax import lax
from jax.sharding import PartitionSpec as P


def shards(
    one_query, other_query, one_key, other_key, one_value, other_value, mix_share, norm_gain
):
    result_query = mix_share[:, None] * one_query + (1.0 - mix_share[:, None]) * other_query
    result_key = mix_share[:, None] * one_key + (1.0 - mix_share[:, None]) * other_key
    result_value = mix_share[:, None] * one_value + (1.0 - mix_share[:, None]) * other_value
    result_gained_query = result_query * norm_gain[:, None]
    result_gained_key = result_key * norm_gain[:, None]
    result_gained_value = result_value * norm_gain[:, None]
    scale_query, scale_key, scale_value = lax.pmax(
        (
            jnp.max(jnp.abs(result_gained_query), axis=0),
            jnp.max(jnp.abs(result_gained_key), axis=0),
            jnp.max(jnp.abs(result_gained_value), axis=0),
        ),
        "shard",
    )
    narrow_query, narrow_key, narrow_value = (
        (result_gained_query / scale_query).astype(jnp.bfloat16),
        (result_gained_key / scale_key).astype(jnp.bfloat16),
        (result_gained_value / scale_value).astype(jnp.bfloat16),
    )
    final_query, final_key, final_value = (
        lax.all_gather(narrow_query, "shard", axis=0, tiled=True),
        lax.all_gather(narrow_key, "shard", axis=0, tiled=True),
        lax.all_gather(narrow_value, "shard", axis=0, tiled=True),
    )
    return (final_query, final_key, final_value, scale_query, scale_key, scale_value)


def solution(mesh):
    placed = (
        P(("job", "shard"), "cols"),
        P(("job", "shard"), "cols"),
        P(("job", "shard"), "cols"),
        P(("job", "shard"), "cols"),
        P(("job", "shard"), "cols"),
        P(("job", "shard"), "cols"),
        P(("job", "shard")),
        P(("job", "shard")),
    )
    return jax.shard_map(
        shards,
        mesh=mesh,
        in_specs=placed,
        out_specs=(
            P("job", "cols"),
            P("job", "cols"),
            P("job", "cols"),
            P(("job", "cols")),
            P(("job", "cols")),
            P(("job", "cols")),
        ),
        check_vma=False,
    )
```

profile of v0, /device:TPU:0, one launch (start us, length us, event | category | flops | bytes accessed | tf_op | source)
XLA Modules:
  0.0 94.1 jit_solution(1859230134611936218)
XLA Ops:
  7.2 0.0 all-gather.6.cloned.1.call-start
  7.2 0.7 broadcast_subtract_fusion
  7.9 0.0 copy-start.2
  7.9 0.0 copy-start.3
  7.9 0.0 copy-start.4
  7.9 0.0 copy-start.5
  7.9 0.0 copy-start.6
  7.9 0.0 copy-start.7
  8.0 10.3 %abs_reduce_fusion = (f32[1024]{0:T(1024)S(1)}, f32[2048,1024]{1,0:T(8,128)}) fusion(f32[2048]{0:T(1024)} %param.15, f32[2048,1024]{1,0:T(8,128)} %param.9, f32[2048]{0:T(1024)S(1)} %broadcast_subtract_fusion, f32[2048,1024]{1,0:T(8,128)} %param.8, f32[2048]{0:T(1024)} %param.14), kind=kLoop, calls=%fused_computation.1 | loop fusion | flops 12581888 | bytes 25194496 | tf_op jit(solution)/shard_map/reduce_max | solution.py:18
  18.3 0.0 copy-done.2
  18.3 0.0 copy-done.3
  18.3 0.0 copy-done.4
  18.3 0.7 copy-done.5
  19.0 0.0 copy-done.6
  19.0 0.0 copy-done.7
  19.0 1.9 %abs_reduce_fusion.1 = (f32[256]{0:T(256)S(1)}, f32[2048,256]{1,0:T(8,128)S(1)}, f32[256]{0:T(256)S(1)}, f32[2048,256]{1,0:T(8,128)}) fusion(f32[2048]{0:T(1024)S(1)} %copy-done.7, f32[2048,256]{1,0:T(8,128)S(1)} %copy-done.2, f32[2048]{0:T(1024)S(1)} %broadcast_subtract_fusion, f32[2048,256]{1,0:T(8,128)S(1)} %copy-done.3, f32[2048]{0:T(1024)S(1)} %copy-done.6, ...), kind=kLoop, calls=%fused_computation.4 | loop fusion | flops 6290944 | bytes 12609536 | tf_op jit(solution)/shard_map/reduce_max | solution.py:20
  21.0 2.6 %all-reduce = (f32[1024]{0:T(1024)S(1)}, f32[256]{0:T(256)S(1)}, f32[256]{0:T(256)S(1)}) all-reduce(f32[1024]{0:T(1024)S(1)} %get-tuple-element.13, f32[256]{0:T(256)S(1)} %get-tuple-element.15, f32[256]{0:T(256)S(1)} %get-tuple-element.9), channel_id=1, replica_groups=mesh['shard'=2,'cols'=4,'job'=4] {'shard'}, use_global_device_ids=true, to_apply=%region_1.0 | all-reduce | flops 1536 | bytes 12288 | tf_op jit(solution)/shard_map/pmax | solution.py:16
  23.6 0.0 copy-start.9
  23.6 0.0 copy-start.10
  23.6 0.0 copy-start.8
  23.6 2.7 %divide_convert_fusion.2 = bf16[2048,256]{1,0:T(8,128)(2,1)} fusion(f32[2048,256]{1,0:T(8,128)} %get-tuple-element.16, f32[256]{0:T(256)S(1)} %get-tuple-element.27), kind=kLoop, calls=%fused_computation.6 | loop fusion | flops 1048576 | bytes 3146752 | tf_op jit(solution)/shard_map/convert_element_type | solution.py:26
  26.3 0.0 all-gather.6.cloned.1.call-update
  26.4 0.0 copy-done.9
  26.4 0.0 all-gather.8.cloned.1.call-start
  26.4 0.0 copy-done.10
  26.4 1.1 %divide_convert_fusion.1 = bf16[2048,256]{1,0:T(8,128)(2,1)} fusion(f32[2048,256]{1,0:T(8,128)S(1)} %get-tuple-element.10, f32[256]{0:T(256)S(1)} %get-tuple-element.28), kind=kLoop, calls=%fused_computation.3 | loop fusion | flops 1048576 | bytes 3146752 | tf_op jit(solution)/shard_map/convert_element_type | solution.py:27
  27.6 0.0 all-gather.8.cloned.1.call-update
  27.6 0.0 all-gather.4.cloned.1.call-start
  27.6 0.0 copy-done.8
  27.6 6.6 %divide_convert_fusion = bf16[2048,1024]{1,0:T(8,128)(2,1)} fusion(f32[2048,1024]{1,0:T(8,128)} %get-tuple-element.14, f32[1024]{0:T(1024)S(1)} %get-tuple-element.26), kind=kLoop, calls=%fused_computation | loop fusion | flops 4194304 | bytes 12587008 | tf_op jit(solution)/shard_map/convert_element_type | solution.py:25
  34.3 0.0 all-gather.4.cloned.1.call-update
  34.3 5.4 %all-gather.6.cloned.1.call-done = bf16[4096,256]{1,0:T(8,128)(2,1)} async-done(((bf16[2048,256]{1,0:T(8,128)(2,1)}), bf16[4096,256]{1,0:T(8,128)(2,1)}) %all-gather.6.cloned.1.call-update) | async-done | bytes 2097168 | tf_op jit(solution)/shard_map/all_gather | solution.py:31
  39.7 0.0 copy-start
  39.7 13.9 %all-gather.8.cloned.1.call-done = bf16[4096,256]{1,0:T(8,128)(2,1)} async-done(((bf16[2048,256]{1,0:T(8,128)(2,1)}), bf16[4096,256]{1,0:T(8,128)(2,1)}) %all-gather.8.cloned.1.call-update) | async-done | bytes 2097168 | tf_op jit(solution)/shard_map/all_gather | solution.py:32
  53.6 22.6 %all-gather.4.cloned.1.call-done = bf16[4096,1024]{1,0:T(8,128)(2,1)} async-done(((bf16[2048,1024]{1,0:T(8,128)(2,1)}), bf16[4096,1024]{1,0:T(8,128)(2,1)}) %all-gather.4.cloned.1.call-update) | async-done | bytes 8388624 | tf_op jit(solution)/shard_map/all_gather | solution.py:30
  76.2 7.8 %copy.17 = bf16[4096,1024]{1,0:T(8,128)(2,1)} copy(bf16[4096,1024]{1,0:T(8,128)(2,1)} %all-gather.4.cloned.1.call-done) | data formatting | bytes 16777216
  83.9 0.0 copy-done
  83.9 0.0 copy-start.1
  83.9 1.3 %copy.18 = bf16[4096,256]{1,0:T(8,128)(2,1)} copy(bf16[4096,256]{1,0:T(8,128)(2,1)S(1)} %copy-done) | data formatting | bytes 4194304
  85.2 1.0 %copy-done.1 = bf16[4096,256]{1,0:T(8,128)(2,1)S(1)} copy-done((bf16[4096,256]{1,0:T(8,128)(2,1)S(1)}, bf16[4096,256]{1,0:T(8,128)(2,1)}, u32[]{:S(2)}) %copy-start.1) | copy-done | bytes 2097176
  86.3 1.3 %copy.19 = bf16[4096,256]{1,0:T(8,128)(2,1)} copy(bf16[4096,256]{1,0:T(8,128)(2,1)S(1)} %copy-done.1) | data formatting | bytes 4194304
Async XLA Ops:
  7.2 32.5 %all-gather.6.cloned.1.call-start = ((), (), s32[]{:S(2)}) async-start(), calls=%async_computation.1 | async-start | bytes 3145728 | tf_op jit(solution)/shard_map/all_gather | solution.py:31
  7.9 10.4 %copy-start.2 = (f32[2048,256]{1,0:T(8,128)S(1)}, f32[2048,256]{1,0:T(8,128)}, u32[]{:S(2)}) copy-start(f32[2048,256]{1,0:T(8,128)} %param.13) | copy-start | bytes 6291460
  7.9 10.4 %copy-start.3 = (f32[2048,256]{1,0:T(8,128)S(1)}, f32[2048,256]{1,0:T(8,128)}, u32[]{:S(2)}) copy-start(f32[2048,256]{1,0:T(8,128)} %param.12) | copy-start | bytes 6291460
  7.9 10.4 %copy-start.4 = (f32[2048,256]{1,0:T(8,128)S(1)}, f32[2048,256]{1,0:T(8,128)}, u32[]{:S(2)}) copy-start(f32[2048,256]{1,0:T(8,128)} %param.11) | copy-start | bytes 6291460
  7.9 11.1 %copy-start.5 = (f32[2048,256]{1,0:T(8,128)S(1)}, f32[2048,256]{1,0:T(8,128)}, u32[]{:S(2)}) copy-start(f32[2048,256]{1,0:T(8,128)} %param.10) | copy-start | bytes 6291460
  7.9 11.1 %copy-start.6 = (f32[2048]{0:T(1024)S(1)}, f32[2048]{0:T(1024)}, u32[]{:S(2)}) copy-start(f32[2048]{0:T(1024)} %param.14) | copy-start | bytes 24580
  7.9 11.1 %copy-start.7 = (f32[2048]{0:T(1024)S(1)}, f32[2048]{0:T(1024)}, u32[]{:S(2)}) copy-start(f32[2048]{0:T(1024)} %param.15) | copy-start | bytes 24580
  23.6 2.8 %copy-start.9 = (f32[256]{0:T(256)}, f32[256]{0:T(256)S(1)}, u32[]{:S(2)}) copy-start(f32[256]{0:T(256)S(1)} %get-tuple-element.27) | copy-start | bytes 3076
  23.6 2.8 %copy-start.10 = (f32[256]{0:T(256)}, f32[256]{0:T(256)S(1)}, u32[]{:S(2)}) copy-start(f32[256]{0:T(256)S(1)} %get-tuple-element.28) | copy-start | bytes 3076
  23.6 4.0 %copy-start.8 = (f32[1024]{0:T(1024)}, f32[1024]{0:T(1024)S(1)}, u32[]{:S(2)}) copy-start(f32[1024]{0:T(1024)S(1)} %get-tuple-element.26) | copy-start | bytes 12292
  26.4 27.2 %all-gather.8.cloned.1.call-start = ((), (), s32[]{:S(2)}) async-start(), calls=%async_computation.2 | async-start | bytes 3145728 | tf_op jit(solution)/shard_map/all_gather | solution.py:32
  27.6 48.6 %all-gather.4.cloned.1.call-start = ((), (), s32[]{:S(2)}) async-start(), calls=%async_computation | async-start | bytes 12582912 | tf_op jit(solution)/shard_map/all_gather | solution.py:30
  39.7 44.3 %copy-start = (bf16[4096,256]{1,0:T(8,128)(2,1)S(1)}, bf16[4096,256]{1,0:T(8,128)(2,1)}, u32[]{:S(2)}) copy-start(bf16[4096,256]{1,0:T(8,128)(2,1)} %all-gather.6.cloned.1.call-done) | copy-start | bytes 6291460
  83.9 2.3 %copy-start.1 = (bf16[4096,256]{1,0:T(8,128)(2,1)S(1)}, bf16[4096,256]{1,0:T(8,128)(2,1)}, u32[]{:S(2)}) copy-start(bf16[4096,256]{1,0:T(8,128)(2,1)} %all-gather.8.cloned.1.call-done) | copy-start | bytes 6291460
Sparse Core Ops, SparseCore 0:
  26.5 13.1 all-gather.5
  41.8 11.7 all-gather.7
  55.1 21.0 all-gather.3
where the time goes:
time: 94.4 us; the launch traced here: 94.1 us
  waiting for transfers between devices  41.9 us (44%)
  other arithmetic  23.5 us (25%)
  between operations  13.8 us (15%)
  local copies, waits for them, and re-layouts  12.2 us (13%)
  blocking collectives  2.62 us (3%)
    all_gather x1, waiting for transfers between devices, shards(): lax.all_gather(narrow_query, 'shard', axis=0, tiled=True)  22.6 us
    all_gather x1, waiting for transfers between devices, shards(): lax.all_gather(narrow_value, 'shard', axis=0, tiled=True)  13.9 us
    unnamed x25, local copies, waits for them, and re-layouts  12.2 us
    reduce_max x1, other arithmetic, shards(): jnp.max(jnp.abs(result_gained_query), axis=0)  10.3 us
    convert_element_type x1, other arithmetic, shards(): (result_gained_query / scale_query).astype(jnp.bfloat16)  6.62 us
    all_gather x1, waiting for transfers between devices, shards(): lax.all_gather(narrow_key, 'shard', axis=0, tiled=True)  5.36 us
    convert_element_type x1, other arithmetic, shards(): (result_gained_key / scale_key).astype(jnp.bfloat16)  2.73 us
    pmax x1, blocking collectives, shards(): lax.pmax((jnp.max(jnp.abs(result_gained_query), axis=0), jnp.max(jnp.abs(...  2.62 us
  transfers between devices with their start and end apart: 3, of which 3 were waited for; matrix products, arithmetic and copies ran while one was open for 8% of the time, Pallas kernels for 0%

commit v1 on v0

--- a/solution.py
+++ b/solution.py
@@ -2,6 +2,11 @@
 import jax.numpy as jnp
 from jax import lax
 from jax.sharding import PartitionSpec as P
+
+
+def gather_over(x, axis, along):
+    sent = jnp.stack([x] * lax.axis_size(axis))
+    return jnp.concatenate(lax.all_to_all(sent, axis, 0, 0), axis=along)
 
 
 def shards(
@@ -27,7 +32,7 @@
         (result_gained_value / scale_value).astype(jnp.bfloat16),
     )
     final_query, final_key, final_value = (
-        lax.all_gather(narrow_query, "shard", axis=0, tiled=True),
+        gather_over(narrow_query, "shard", 0),
         lax.all_gather(narrow_key, "shard", axis=0, tiled=True),
         lax.all_gather(narrow_value, "shard", axis=0, tiled=True),
     )

time: 94.4 us -> 75.9 us (0.80)
  waiting for transfers between devices: 41.9 us -> 0.04 us
  blocking collectives: 2.62 us -> 22.6 us
  other arithmetic: 23.5 us -> 25.6 us
    all_gather x1 -> x0, waiting for transfers between devices: 22.6 us -> none  [shards(): lax.all_gather(narrow_query, 'shard', axis=0, tiled=True)]
    all_to_all x0 -> x1, blocking collectives: none -> 20 us  [gather_over(): return jnp.concatenate(lax.all_to_all(sent, axis, 0, 0), axis=along)]
    all_gather x1, waiting for transfers between devices: 13.9 us -> 0.01 us  [shards(): lax.all_gather(narrow_value, 'shard', axis=0, tiled=True)]
    another operation x0 -> x2, other arithmetic: none -> 8.79 us  [gather_over(): sent = jnp.stack([x] * lax.axis_size(axis))]
    convert_element_type x1 -> x0, other arithmetic: 6.62 us -> none  [shards(): (result_gained_query / scale_query).astype(jnp.bfloat16)]
    all_gather x1, waiting for transfers between devices: 5.36 us -> 0.01 us  [shards(): lax.all_gather(narrow_key, 'shard', axis=0, tiled=True)]
  transfers between devices with their start and end apart: 3 -> 2, of which waited for: 3 -> 0; matrix products, arithmetic and copies ran while one was open for 8% -> 13% of each run, Pallas kernels for 0% -> 0%
where the time goes in v1:
time: 75.9 us; the launch traced here: 74.8 us
  other arithmetic  25.6 us (34%)
  blocking collectives  22.6 us (30%)
  between operations  14.1 us (19%)
  local copies, waits for them, and re-layouts  12.3 us (16%)
    all_to_all x1, blocking collectives, gather_over(): return jnp.concatenate(lax.all_to_all(sent, axis, 0, 0), axis=along)  20 us
    unnamed x25, local copies, waits for them, and re-layouts  12.3 us
    reduce_max x1, other arithmetic, shards(): jnp.max(jnp.abs(result_gained_query), axis=0)  10.3 us
    another operation x2, other arithmetic, gather_over(): sent = jnp.stack([x] * lax.axis_size(axis))  8.79 us
    convert_element_type x1, other arithmetic, shards(): (result_gained_key / scale_key).astype(jnp.bfloat16)  2.73 us
    pmax x1, blocking collectives, shards(): lax.pmax((jnp.max(jnp.abs(result_gained_query), axis=0), jnp.max(jnp.abs(...  2.62 us
    reduce_max x1, other arithmetic, shards(): jnp.max(jnp.abs(result_gained_value), axis=0)  1.95 us
  transfers between devices with their start and end apart: 2, of which 0 were waited for; matrix products, arithmetic and copies ran while one was open for 13% of the time, Pallas kernels for 0%

profile of v1, /device:TPU:0, one launch (start us, length us, event | category | flops | bytes accessed | tf_op | source)
XLA Modules:
  0.0 74.8 jit_solution(5938234592312448090)
XLA Ops:
  7.2 0.0 all-gather.3.cloned.1.call-start
  7.2 0.7 broadcast_subtract_fusion
  7.9 0.0 copy-start.2
  7.9 0.0 copy-start.3
  7.9 0.0 copy-start.4
  7.9 0.0 copy-start.5
  7.9 0.0 copy-start.6
  7.9 0.0 copy-start.7
  8.0 10.3 %abs_reduce_fusion = (f32[1024]{0:T(1024)S(1)}, f32[2048,1024]{1,0:T(8,128)}) fusion(f32[2048]{0:T(1024)} %param.15, f32[2048,1024]{1,0:T(8,128)} %param.9, f32[2048]{0:T(1024)S(1)} %broadcast_subtract_fusion, f32[2048,1024]{1,0:T(8,128)} %param.8, f32[2048]{0:T(1024)} %param.14), kind=kLoop, calls=%fused_computation.2 | loop fusion | flops 12581888 | bytes 25194496 | tf_op jit(solution)/shard_map/reduce_max | solution.py:23
  18.3 0.0 copy-done.2
  18.3 0.0 copy-done.3
  18.3 0.0 copy-done.4
  18.3 0.7 copy-done.5
  19.0 0.0 copy-done.6
  19.0 0.0 copy-done.7
  19.0 1.9 %abs_reduce_fusion.1 = (f32[256]{0:T(256)S(1)}, f32[2048,256]{1,0:T(8,128)S(1)}, f32[256]{0:T(256)S(1)}, f32[2048,256]{1,0:T(8,128)}) fusion(f32[2048]{0:T(1024)S(1)} %copy-done.7, f32[2048,256]{1,0:T(8,128)S(1)} %copy-done.2, f32[2048]{0:T(1024)S(1)} %broadcast_subtract_fusion, f32[2048,256]{1,0:T(8,128)S(1)} %copy-done.3, f32[2048]{0:T(1024)S(1)} %copy-done.6, ...), kind=kLoop, calls=%fused_computation.6 | loop fusion | flops 6290944 | bytes 12609536 | tf_op jit(solution)/shard_map/reduce_max | solution.py:25
  21.0 2.6 %all-reduce = (f32[1024]{0:T(1024)S(1)}, f32[256]{0:T(256)S(1)}, f32[256]{0:T(256)S(1)}) all-reduce(f32[1024]{0:T(1024)S(1)} %get-tuple-element.13, f32[256]{0:T(256)S(1)} %get-tuple-element.15, f32[256]{0:T(256)S(1)} %get-tuple-element.9), channel_id=1, replica_groups=mesh['shard'=2,'cols'=4,'job'=4] {'shard'}, use_global_device_ids=true, to_apply=%region_1.0 | all-reduce | flops 1536 | bytes 12288 | tf_op jit(solution)/shard_map/pmax | solution.py:21
  23.6 0.0 copy-start.9
  23.6 0.0 copy-start.10
  23.6 0.0 copy-start.8
  23.6 2.7 %divide_convert_fusion.2 = bf16[2048,256]{1,0:T(8,128)(2,1)} fusion(f32[2048,256]{1,0:T(8,128)} %get-tuple-element.16, f32[256]{0:T(256)S(1)} %get-tuple-element.27), kind=kLoop, calls=%fused_computation.8 | loop fusion | flops 1048576 | bytes 3146752 | tf_op jit(solution)/shard_map/convert_element_type | solution.py:31
  26.3 0.0 all-gather.3.cloned.1.call-update
  26.4 0.0 copy-done.9
  26.4 0.0 all-gather.5.cloned.1.call-start
  26.4 0.0 copy-done.10
  26.4 1.1 %divide_convert_fusion.1 = bf16[2048,256]{1,0:T(8,128)(2,1)} fusion(f32[2048,256]{1,0:T(8,128)S(1)} %get-tuple-element.10, f32[256]{0:T(256)S(1)} %get-tuple-element.28), kind=kLoop, calls=%fused_computation.5 | loop fusion | flops 1048576 | bytes 3146752 | tf_op jit(solution)/shard_map/convert_element_type | solution.py:32
  27.6 0.0 all-gather.5.cloned.1.call-update
  27.6 0.0 copy-done.8
  27.6 4.6 %fusion = bf16[1,2048,1024]{2,1,0:T(8,128)(2,1)S(1)} fusion(f32[2048,1024]{1,0:T(8,128)} %get-tuple-element.14, f32[1024]{0:T(1024)S(1)} %get-tuple-element.26), kind=kLoop, calls=%fused_computation.4 | loop fusion | flops 4194304 | bytes 12587008 | tf_op jit(solution)/shard_map/stack | solution.py:8
  32.3 4.1 %pad_maximum_fusion = bf16[2,2048,1024]{2,1,0:T(8,128)(2,1)} fusion(bf16[1,2048,1024]{2,1,0:T(8,128)(2,1)S(1)} %fusion), kind=kLoop, calls=%fused_computation | loop fusion | flops 4194304 | bytes 12582912 | tf_op jit(solution)/shard_map/stack | solution.py:8
  36.4 20.0 %all_to_all.5 = bf16[2,2048,1024]{2,1,0:T(8,128)(2,1)} all-to-all(bf16[2,2048,1024]{2,1,0:T(8,128)(2,1)} %pad_maximum_fusion), channel_id=1, replica_groups=mesh['shard'=2,'cols'=4,'job'=4] {'shard'}, dimensions={0} | all-to-all | bytes 16777216 | tf_op jit(solution)/shard_map/all_to_all | solution.py:9
  56.4 0.0 all-gather.3.cloned.1.call-done
  56.4 0.0 copy-start
  56.4 0.0 all-gather.5.cloned.1.call-done
  56.4 7.9 %copy.17 = bf16[4096,1024]{1,0:T(8,128)(2,1)} copy(bf16[4096,1024]{1,0:T(8,128)(2,1)} %bitcast.3) | data formatting | bytes 16777216
  64.3 0.0 copy-done
  64.3 0.0 copy-start.1
  64.3 1.3 %copy.18 = bf16[4096,256]{1,0:T(8,128)(2,1)} copy(bf16[4096,256]{1,0:T(8,128)(2,1)S(1)} %copy-done) | data formatting | bytes 4194304
  65.6 1.0 %copy-done.1 = bf16[4096,256]{1,0:T(8,128)(2,1)S(1)} copy-done((bf16[4096,256]{1,0:T(8,128)(2,1)S(1)}, bf16[4096,256]{1,0:T(8,128)(2,1)}, u32[]{:S(2)}) %copy-start.1) | copy-done | bytes 2097176
  66.6 1.3 %copy.19 = bf16[4096,256]{1,0:T(8,128)(2,1)} copy(bf16[4096,256]{1,0:T(8,128)(2,1)S(1)} %copy-done.1) | data formatting | bytes 4194304
Async XLA Ops:
  7.2 49.2 %all-gather.3.cloned.1.call-start = ((), (), s32[]{:S(2)}) async-start(), calls=%async_computation.1 | async-start | bytes 3145728 | tf_op jit(solution)/shard_map/all_gather | solution.py:36
  7.9 10.4 %copy-start.2 = (f32[2048,256]{1,0:T(8,128)S(1)}, f32[2048,256]{1,0:T(8,128)}, u32[]{:S(2)}) copy-start(f32[2048,256]{1,0:T(8,128)} %param.13) | copy-start | bytes 6291460
  7.9 10.4 %copy-start.3 = (f32[2048,256]{1,0:T(8,128)S(1)}, f32[2048,256]{1,0:T(8,128)}, u32[]{:S(2)}) copy-start(f32[2048,256]{1,0:T(8,128)} %param.12) | copy-start | bytes 6291460
  7.9 10.4 %copy-start.4 = (f32[2048,256]{1,0:T(8,128)S(1)}, f32[2048,256]{1,0:T(8,128)}, u32[]{:S(2)}) copy-start(f32[2048,256]{1,0:T(8,128)} %param.11) | copy-start | bytes 6291460
  7.9 11.1 %copy-start.5 = (f32[2048,256]{1,0:T(8,128)S(1)}, f32[2048,256]{1,0:T(8,128)}, u32[]{:S(2)}) copy-start(f32[2048,256]{1,0:T(8,128)} %param.10) | copy-start | bytes 6291460
  7.9 11.1 %copy-start.6 = (f32[2048]{0:T(1024)S(1)}, f32[2048]{0:T(1024)}, u32[]{:S(2)}) copy-start(f32[2048]{0:T(1024)} %param.14) | copy-start | bytes 24580
  7.9 11.1 %copy-start.7 = (f32[2048]{0:T(1024)S(1)}, f32[2048]{0:T(1024)}, u32[]{:S(2)}) copy-start(f32[2048]{0:T(1024)} %param.15) | copy-start | bytes 24580
  23.6 2.8 %copy-start.9 = (f32[256]{0:T(256)}, f32[256]{0:T(256)S(1)}, u32[]{:S(2)}) copy-start(f32[256]{0:T(256)S(1)} %get-tuple-element.27) | copy-start | bytes 3076
  23.6 2.8 %copy-start.10 = (f32[256]{0:T(256)}, f32[256]{0:T(256)S(1)}, u32[]{:S(2)}) copy-start(f32[256]{0:T(256)S(1)} %get-tuple-element.28) | copy-start | bytes 3076
  23.6 4.0 %copy-start.8 = (f32[1024]{0:T(1024)}, f32[1024]{0:T(1024)S(1)}, u32[]{:S(2)}) copy-start(f32[1024]{0:T(1024)S(1)} %get-tuple-element.26) | copy-start | bytes 12292
  26.4 30.0 %all-gather.5.cloned.1.call-start = ((), (), s32[]{:S(2)}) async-start(), calls=%async_computation.2 | async-start | bytes 3145728 | tf_op jit(solution)/shard_map/all_gather | solution.py:37
  56.4 7.9 %copy-start = (bf16[4096,256]{1,0:T(8,128)(2,1)S(1)}, bf16[4096,256]{1,0:T(8,128)(2,1)}, u32[]{:S(2)}) copy-start(bf16[4096,256]{1,0:T(8,128)(2,1)} %all-gather.3.cloned.1.call-done) | copy-start | bytes 6291460
  64.3 2.3 %copy-start.1 = (bf16[4096,256]{1,0:T(8,128)(2,1)S(1)}, bf16[4096,256]{1,0:T(8,128)(2,1)}, u32[]{:S(2)}) copy-start(bf16[4096,256]{1,0:T(8,128)(2,1)} %all-gather.5.cloned.1.call-done) | copy-start | bytes 6291460
Sparse Core Ops, SparseCore 0:
  26.5 13.1 all-gather.2
  41.8 13.0 all-gather.4
